TPU v7x, 256 devices: a 8x8x2 block of a 8x8x16 slice. The times are simulated.
256 devices in a mesh: group: 2 (over z), dp: 16 (over y, core), tensor: 8 (over x).
Axes of the slice: x: 8, y: 8, z: 2, core: 2. Of those that a mesh axis runs over, the one named last changes fastest.
The devices are a block of a 8x8x16 slice.
Arguments:
- tokens: bfloat16 [4096, 5120], P(('group', 'dp'), 'tensor'), parts along dimension 0, may hold values from -6 to 6
- router: bfloat16 [5120, 8], replicated, may hold values from -0.078125 to 0.078125
- expert_gate: bfloat16 [5120, 32768], P(None, ('dp', 'tensor')), may hold values from -0.078125 to 0.078125
- expert_up: bfloat16 [5120, 32768], P(None, ('dp', 'tensor')), may hold values from -0.078125 to 0.078125
- expert_down: bfloat16 [32768, 5120], P(('dp', 'tensor')), may hold values from -0.09375 to 0.09375
- shared_gate: bfloat16 [5120, 4096], P('dp', 'tensor'), may hold values from -0.078125 to 0.078125
- shared_up: bfloat16 [5120, 4096], P('dp', 'tensor'), may hold values from -0.078125 to 0.078125
- shared_down: bfloat16 [4096, 5120], P('tensor', 'dp'), may hold values from -0.09375 to 0.09375
- expert_ids: int32 [4096], P(('group', 'dp')), parts along dimension 0, may hold values from 0 to 7, as said below
- expert_slots: int32 [4096], P(('group', 'dp')), parts along dimension 0, may hold values from 0 to 31, as said below
Outputs:
- mixed: bfloat16 [4096, 5120], P(('group', 'dp'), 'tensor'), parts along dimension 0
There are 2 independent parts, one for each index of `group`. A program takes and returns all parts, laid end to end along the dimension named above; an argument that names none is the same for every part. Nothing has to cross between parts.
Inputs may be any that keep to these rules, and one draw needn't show every extreme that they name: `expert_ids`: among the tokens of one index of dp no expert has more than 32; in every draw one expert has exactly 32 tokens from every index of dp. `expert_slots`: tokens of one index of dp with the same expert have distinct slots.
All inputs are finite; a program needn't handle non-finite values.
Results may differ from a plain program's by a relative error of at most 0.015.
Values may be sent and summed in bfloat16 or wider, within the bound.
No kernel may reach another device: no remote copies, remote signals or barrier semaphores. Data moves between devices by JAX's collectives and lax.ppermute only.
A program may use at most 128 MiB of HBM per device.

v0:
```python
import jax
import jax.numpy as jnp
from jax import lax
from jax.sharding import PartitionSpec as P


def joined_along(tiles, dim):
    dims = list(tiles.shape[1:])
    dims[dim] *= tiles.shape[0]
    return jnp.moveaxis(tiles, 0, dim).reshape(dims)


def copy_for_each(value, axis):
    copies = jnp.broadcast_to(value, (lax.axis_size(axis), *value.shape))
    return lax.all_to_all(copies, axis, split_axis=0, concat_axis=0, tiled=True)


def gather_directly(value, axis, dim):
    return joined_along(copy_for_each(value, axis), dim)


def side_by_side(arrays, axis, dim, along):
    both = jnp.concatenate(arrays, axis=along)
    out, at, finished = (lax.all_gather(both, axis, axis=dim, tiled=True), 0, [])
    for a in arrays:
        finished.append(lax.slice_in_dim(out, at, at + a.shape[along], axis=along))
        at += a.shape[along]
    return tuple(finished)


def split_up(value, dim, devices):
    before, after = (value.shape[:dim], value.shape[dim + 1 :])
    return jnp.moveaxis(value.reshape(*before, devices, -1, *after), dim, 0)


def sum_at_owner(value, axis, dim):
    tiles = split_up(value, dim, lax.axis_size(axis))
    arrived = lax.all_to_all(tiles, axis, split_axis=0, concat_axis=0, tiled=True)
    return arrived.astype(jnp.float32).sum(axis=0)


def swapped(value, axis, bit):
    mask = 2**bit
    pairs = [(source, source ^ mask) for source in range(lax.axis_size(axis))]
    return lax.ppermute(value, axis, pairs)


def on_device(
    tokens,
    router,
    expert_gate,
    expert_up,
    expert_down,
    shared_gate,
    shared_up,
    shared_down,
    expert_ids,
    expert_slots,
):
    tok_rows, part_width = tokens.shape
    dp_count = lax.axis_size("dp")
    experts = dp_count // 2
    capacity = min(2 * tok_rows // experts, tok_rows // 2)
    gathered = gather_directly(tokens, "tensor", 1)
    logits = jnp.dot(gathered, router, preferred_element_type=jnp.float32)
    one_hot = (expert_ids[:, None] == jnp.arange(experts, dtype=jnp.int32)[None, :]).astype(
        jnp.float32
    )
    gating = jax.nn.sigmoid(jnp.sum(logits * one_hot, axis=1))
    routed = (tokens.astype(jnp.float32) * gating[:, None]).astype(jnp.bfloat16)
    outgoing = (
        jnp.zeros((experts, capacity, part_width), jnp.bfloat16)
        .at[expert_ids, expert_slots]
        .set(routed)
    )
    pieces = side_by_side((shared_gate, shared_up), "dp", 0, 1)
    gate_sum = jnp.dot(gathered, pieces[0], preferred_element_type=jnp.float32)
    up_sum = jnp.dot(gathered, pieces[1], preferred_element_type=jnp.float32)
    shared_hidden = (jax.nn.silu(gate_sum) * up_sum).astype(jnp.bfloat16)
    shared_terms = jnp.dot(
        shared_hidden,
        lax.all_gather(shared_down, "dp", axis=1, tiled=True),
        preferred_element_type=jnp.float32,
    )
    shared_out = lax.psum_scatter(
        shared_terms.astype(jnp.bfloat16), "tensor", scatter_dimension=1, tiled=True
    ).astype(jnp.float32)
    half_cap = capacity // 2
    to_send = outgoing.reshape(dp_count, half_cap, part_width)
    own_half = lax.all_to_all(to_send, "dp", split_axis=0, concat_axis=0, tiled=True)
    partner = swapped(own_half, "dp", 0)
    parity = lax.axis_index("dp") % 2
    odd_host = parity == 1
    lower_half = jnp.where(odd_host, partner, own_half)
    upper_half = jnp.where(odd_host, own_half, partner)
    received = jnp.concatenate([lower_half, upper_half], axis=1)
    source_count = received.shape[0]
    slot_count = received.shape[1]
    slot_total = source_count * slot_count
    portion = lax.all_gather(received, "tensor", axis=2, tiled=True)
    flattened = portion.reshape(slot_total, portion.shape[2])
    gate_e = jnp.dot(flattened, expert_gate, preferred_element_type=jnp.float32)
    up_e = jnp.dot(flattened, expert_up, preferred_element_type=jnp.float32)
    hidden_e = (jax.nn.silu(gate_e) * up_e).astype(jnp.bfloat16)
    expert_terms = jnp.dot(hidden_e, expert_down, preferred_element_type=jnp.float32)
    expert_terms = expert_terms.reshape(source_count, slot_count, expert_terms.shape[1])
    partials = sum_at_owner(expert_terms.astype(jnp.bfloat16), "tensor", 2)
    partner_sum = swapped(partials.astype(jnp.bfloat16), "dp", 0).astype(partials.dtype)
    paired = partials + partner_sum
    kept_half = lax.dynamic_slice_in_dim(paired, parity * half_cap, half_cap, 1).astype(
        jnp.bfloat16
    )
    returned_raw = lax.all_to_all(kept_half, "dp", split_axis=0, concat_axis=0, tiled=True)
    returned = returned_raw.reshape(experts, capacity, part_width)
    expert_out = returned[expert_ids, expert_slots]
    return (shared_out + expert_out.astype(jnp.float32)).astype(jnp.bfloat16)


def solution(mesh):
    in_specs = (
        P(("group", "dp"), "tensor"),
        P(),
        P(None, ("dp", "tensor")),
        P(None, ("dp", "tensor")),
        P(("dp", "tensor"), None),
        P("dp", "tensor"),
        P("dp", "tensor"),
        P("tensor", "dp"),
        P(("group", "dp")),
        P(("group", "dp")),
    )
    out_specs = P(("group", "dp"), "tensor")
    return jax.shard_map(
        on_device, mesh=mesh, in_specs=in_specs, out_specs=out_specs, check_vma=False
    )
```

profile of v0, /device:TPU:515, one launch (start us, length us, event | category | flops | bytes accessed | tf_op | source)
XLA Modules:
  0.0 342.5 jit_solution(5509344661017308061)
XLA Ops:
  6.6 1.2 copy.12
  7.8 1.3 broadcast_in_dim.8
  9.0 7.2 %all-to-all-start = ((bf16[8,128,640]{1,2,0:T(8,128)(2,1)}), bf16[8,128,640]{1,2,0:T(8,128)(2,1)}, u32[]{:S(2)}, u32[]{:S(2)}) async-start(bf16[8,128,640]{1,2,0:T(8,128)(2,1)} %broadcast_in_dim.8), calls=%async_computation | async-start | bytes 2621440 | tf_op jit(solution)/shard_map/all_to_all | solution.py:15
  16.2 19.5 %all-to-all-done = bf16[8,128,640]{1,2,0:T(8,128)(2,1)} async-done(((bf16[8,128,640]{1,2,0:T(8,128)(2,1)}), bf16[8,128,640]{1,2,0:T(8,128)(2,1)}, u32[]{:S(2)}, u32[]{:S(2)}) %all-to-all-start) | async-done | bytes 1310752 | tf_op jit(solution)/shard_map/all_to_all | solution.py:15
  35.7 1.6 fusion.17
  37.5 8.0 %scatter_fusion = bf16[8,32,640]{2,1,0:T(8,128)(2,1)S(1)} fusion(bf16[8,32,640]{2,1,0:T(8,128)(2,1)S(1)} %broadcast_in_dim.18, s32[128]{0:T(128)S(1)} %get-tuple-element.8, bf16[128,640]{1,0:T(8,128)(2,1)S(1)} %multiply_convert_fusion), kind=kCustom, calls=%fused_computation.1 | custom fusion | bytes 492544 | tf_op jit(solution)/shard_map/scatter | solution.py:74
  45.5 40.7 %all_to_all.20 = bf16[16,16,640]{2,1,0:T(8,128)(2,1)S(1)} all-to-all(bf16[16,16,640]{2,1,0:T(8,128)(2,1)S(1)} %bitcast.60), channel_id=1, replica_groups=mesh['group'=2,'dp'=16,'tensor'=8] {'dp'}, dimensions={0} | all-to-all | bytes 655360 | tf_op jit(solution)/shard_map/all_to_all | solution.py:90
  86.2 1.6 collective-permute-done
  87.9 0.9 pad_maximum_fusion.1
  88.9 2.0 pad_maximum_fusion
  91.0 0.7 all-gather.6.cloned.1.call-update
  91.7 63.9 %all-gather.8.cloned.1.call-done = bf16[16,32,5120]{2,1,0:T(8,128)(2,1)} async-done(((bf16[16,32,640]{2,1,0:T(8,128)(2,1)}), bf16[16,32,5120]{2,1,0:T(8,128)(2,1)}) %all-gather.8.cloned.1.call-update) | async-done | bytes 5242896 | tf_op jit(solution)/shard_map/all_gather | solution.py:100
  155.6 4.8 %fusion.40 = f32[512,256]{1,0:T(8,128)S(1)} fusion(bf16[512,5120]{1,0:T(8,128)(2,1)} %bitcast.65, bf16[5120,256]{1,0:T(8,128)(2,1)} %param.12), kind=kOutput, calls=%fused_computation.52 | convolution fusion | flops 1342177280 | bytes 8388608 | tf_op jit(solution)/shard_map/dot_general | solution.py:102
  160.5 11.2 %convolution_convert_fusion = bf16[512,5120]{1,0:T(8,128)(2,1)} fusion(bf16[256,5120]{1,0:T(8,128)(2,1)S(1)} %copy-done, bf16[512,5120]{1,0:T(8,128)(2,1)} %bitcast.66, bf16[5120,256]{1,0:T(8,128)(2,1)} %param.13, f32[512,256]{1,0:T(8,128)S(1)} %fusion.40), kind=kOutput, calls=%fused_computation.3 | convolution fusion | flops 2687762432 | bytes 16252928 | tf_op jit(solution)/shard_map/dot_general | solution.py:105
  171.7 3.7 %copy.16 = bf16[64,8,8,640]{3,2,1,0:T(8,128)(2,1)S(1)} copy(bf16[64,8,8,640]{3,1,2,0:T(8,128)(2,1)} %bitcast.62) | data formatting | bytes 10485760
  175.3 3.1 copy.18
  178.4 6.2 %all-to-all-start.2 = ((bf16[8,16,32,640]{3,2,1,0:T(8,128)(2,1)}), bf16[8,16,32,640]{3,2,1,0:T(8,128)(2,1)}, u32[]{:S(2)}, u32[]{:S(2)}) async-start(bf16[8,16,32,640]{3,2,1,0:T(8,128)(2,1)} %bitcast.58), calls=%async_computation.2 | async-start | bytes 10485760 | tf_op jit(solution)/shard_map/all_to_all | solution.py:38
  184.6 41.0 %all-gather.4.cloned.1.call-done = bf16[5120,1024]{1,0:T(8,128)(2,1)} async-done(((bf16[320,1024]{1,0:T(8,128)(2,1)}), bf16[5120,1024]{1,0:T(8,128)(2,1)}) %all-gather.4.cloned.1.call-update) | async-done | bytes 10485776 | tf_op jit(solution)/shard_map/all_gather | solution.py:24
  225.6 4.4 %fusion.5 = f32[128,512]{0,1:T(8,128)S(1)} fusion(bf16[128,5120]{0,1:T(8,128)(2,1)} %bitcast.1, bf16[5120,1024]{1,0:T(8,128)(2,1)} %all-gather.4.cloned.1.call-done), kind=kOutput, calls=%fused_computation.12 | convolution fusion | flops 671088640 | bytes 6815744 | tf_op jit(solution)/shard_map/dot_general | solution.py:77
  230.1 40.7 %all-gather.6.cloned.1.call-done = bf16[512,5120]{0,1:T(8,128)(2,1)} async-done(((bf16[512,320]{0,1:T(8,128)(2,1)}), bf16[512,5120]{0,1:T(8,128)(2,1)}) %all-gather.6.cloned.1.call-update) | async-done | bytes 5242896 | tf_op jit(solution)/shard_map/all_gather | solution.py:82
  270.7 11.2 %convolution_convert_fusion.1 = bf16[128,5120]{1,0:T(8,128)(2,1)} fusion(bf16[512,5120]{0,1:T(8,128)(2,1)} %all-gather.6.cloned.1.call-done, bf16[128,5120]{0,1:T(8,128)(2,1)} %bitcast.1, bf16[5120,1024]{1,0:T(8,128)(2,1)} %all-gather.4.cloned.1.call-done, f32[128,512]{0,1:T(8,128)S(1)} %fusion.5), kind=kOutput, calls=%fused_computation.4 | convolution fusion | flops 1343225856 | bytes 13369344 | tf_op jit(solution)/shard_map/dot_general | solution.py:80
  281.9 2.4 copy.14
  284.4 17.9 %all-to-all-done.2 = bf16[8,16,32,640]{3,2,1,0:T(8,128)(2,1)} async-done(((bf16[8,16,32,640]{3,2,1,0:T(8,128)(2,1)}), bf16[8,16,32,640]{3,2,1,0:T(8,128)(2,1)}, u32[]{:S(2)}, u32[]{:S(2)}) %all-to-all-start.2) | async-done | bytes 5242912 | tf_op jit(solution)/shard_map/all_to_all | solution.py:38
  302.4 3.4 %convert_reduce_fusion = f32[16,32,640]{2,1,0:T(8,128)S(1)} fusion(bf16[8,16,32,640]{3,2,1,0:T(8,128)(2,1)} %all-to-all-done.2), kind=kLoop, calls=%fused_computation.2 | loop fusion | flops 4915200 | bytes 6553600 | tf_op jit(solution)/shard_map/reduce_sum | solution.py:39
  305.8 1.1 copy-done.1
  307.0 2.7 collective-permute-start.1
  309.7 1.9 collective-permute-done.1
  311.5 2.0 fusion.20
  313.5 7.4 %all-to-all-start.3 = ((bf16[16,16,640]{2,1,0:T(8,128)(2,1)}), bf16[16,16,640]{2,1,0:T(8,128)(2,1)S(1)}, u32[]{:S(2)}, u32[]{:S(2)}) async-start(bf16[16,16,640]{2,1,0:T(8,128)(2,1)} %fusion.20), calls=%async_computation.3 | async-start | bytes 655360 | tf_op jit(solution)/shard_map/all_to_all | solution.py:113
  320.9 1.1 copy.15
  322.0 11.9 %all-to-all-done.3 = bf16[16,16,640]{2,1,0:T(8,128)(2,1)S(1)} async-done(((bf16[16,16,640]{2,1,0:T(8,128)(2,1)}), bf16[16,16,640]{2,1,0:T(8,128)(2,1)S(1)}, u32[]{:S(2)}, u32[]{:S(2)}) %all-to-all-start.3) | async-done | bytes 327712 | tf_op jit(solution)/shard_map/all_to_all | solution.py:113
  333.9 1.4 gather_fusion
  (27 shorter events, 1.3 us)
Async XLA Ops:
  6.5 153.9 %copy-start = (bf16[256,5120]{1,0:T(8,128)(2,1)S(1)}, bf16[256,5120]{1,0:T(8,128)(2,1)}, u32[]{:S(2)}) copy-start(bf16[256,5120]{1,0:T(8,128)(2,1)} %param.14) | copy-start | bytes 7864324
  6.6 9.7 %copy-start.4 = (s32[128]{0:T(128)S(1)}, s32[128]{0:T(128)}, u32[]{:S(2)}) copy-start(s32[128]{0:T(128)} %param.18) | copy-start | bytes 1540
  6.6 9.7 %copy-start.5 = (s32[128]{0:T(128)S(1)}, s32[128]{0:T(128)}, u32[]{:S(2)}) copy-start(s32[128]{0:T(128)} %param.19) | copy-start | bytes 1540
  6.6 29.1 %copy-start.3 = (bf16[5120,8]{0,1:T(8,128)(2,1)S(1)}, bf16[5120,8]{0,1:T(8,128)(2,1)}, u32[]{:S(2)}) copy-start(bf16[5120,8]{0,1:T(8,128)(2,1)} %param.11) | copy-start | bytes 245764
  7.8 29.5 %copy-start.2 = (bf16[128,640]{1,0:T(8,128)(2,1)S(1)}, bf16[128,640]{1,0:T(8,128)(2,1)}, u32[]{:S(2)}) copy-start(bf16[128,640]{1,0:T(8,128)(2,1)} %param.10) | copy-start | bytes 491524
  9.0 26.6 %all-to-all-start = ((bf16[8,128,640]{1,2,0:T(8,128)(2,1)}), bf16[8,128,640]{1,2,0:T(8,128)(2,1)}, u32[]{:S(2)}, u32[]{:S(2)}) async-start(bf16[8,128,640]{1,2,0:T(8,128)(2,1)} %broadcast_in_dim.8), calls=%async_computation | async-start | bytes 2621440 | tf_op jit(solution)/shard_map/all_to_all | solution.py:15
  16.2 139.4 %all-gather.8.cloned.1.call-start = ((), (), s32[]{:S(2)}) async-start(), calls=%async_computation.7 | async-start | bytes 5898240 | tf_op jit(solution)/shard_map/all_gather | solution.py:100
  86.2 1.6 collective-permute-start
  88.8 136.8 %all-gather.4.cloned.1.call-start = ((), (), s32[]{:S(2)}) async-start(), calls=%async_computation.5 | async-start | bytes 11141120 | tf_op jit(solution)/shard_map/all_gather | solution.py:24
  90.9 179.8 %all-gather.6.cloned.1.call-start = ((), (), s32[]{:S(2)}) async-start(), calls=%async_computation.6 | async-start | bytes 5570560 | tf_op jit(solution)/shard_map/all_gather | solution.py:82
  178.4 124.0 %all-to-all-start.2 = ((bf16[8,16,32,640]{3,2,1,0:T(8,128)(2,1)}), bf16[8,16,32,640]{3,2,1,0:T(8,128)(2,1)}, u32[]{:S(2)}, u32[]{:S(2)}) async-start(bf16[8,16,32,640]{3,2,1,0:T(8,128)(2,1)} %bitcast.58), calls=%async_computation.2 | async-start | bytes 10485760 | tf_op jit(solution)/shard_map/all_to_all | solution.py:38
  184.6 136.3 %reduce-scatter.4.cloned.1.call-start = ((), (), s32[]{:S(2)}) async-start(), calls=%async_computation.8 | async-start | bytes 1474560
  305.8 1.1 copy-start.1
  307.0 4.6 %collective-permute-start.1 = (bf16[16,32,640]{2,1,0:T(8,128)(2,1)S(1)}, bf16[16,32,640]{2,1,0:T(8,128)(2,1)}, u32[]{:S(2)}, u32[]{:S(2)}) collective-permute-start(bf16[16,32,640]{2,1,0:T(8,128)(2,1)S(1)} %convert_element_type.53), channel_id=1, source_target_pairs={{0,8},{8,0},{16,24},{24,16},{32,40},{40,32},{48,56},{56,48},{64,72... | collective-permute-start | bytes 1966088 | tf_op jit(solution)/shard_map/ppermute | solution.py:45
  313.5 20.4 %all-to-all-start.3 = ((bf16[16,16,640]{2,1,0:T(8,128)(2,1)}), bf16[16,16,640]{2,1,0:T(8,128)(2,1)S(1)}, u32[]{:S(2)}, u32[]{:S(2)}) async-start(bf16[16,16,640]{2,1,0:T(8,128)(2,1)} %fusion.20), calls=%async_computation.3 | async-start | bytes 655360 | tf_op jit(solution)/shard_map/all_to_all | solution.py:113
Sparse Core Ops, SparseCore 0:
  88.9 66.6 all-gather.7
  157.5 68.1 all-gather.3
  227.5 43.1 all-gather.5
  284.5 36.2 reduce-scatter.3
where the time goes:
time: 343 us
  waiting for transfers between devices  199 us (58%)
  blocking collectives  40.7 us (12%)
  matrix products  33.2 us (10%)
  starting transfers between devices  23.6 us (7%)
  local copies, waits for them, and re-layouts  23.2 us (7%)
  between operations  13.3 us (4%)
  other arithmetic  9.27 us (3%)
    all_gather x1, waiting for transfers between devices, on_device(): portion = lax.all_gather(received, 'tensor', axis=2, tiled=True)  63.9 us
    all_gather x1, waiting for transfers between devices, side_by_side(): lax.all_gather(both, axis, axis=dim, tiled=True)  41 us
    all_to_all x1, blocking collectives, on_device(): lax.all_to_all(to_send, 'dp', split_axis=0, concat_axis=0, tiled=True)  40.7 us
    all_gather x1, waiting for transfers between devices, on_device(): lax.all_gather(shared_down, 'dp', axis=1, tiled=True)  40.7 us
    all_to_all x1, waiting for transfers between devices, copy_for_each(): return lax.all_to_all(copies, axis, split_axis=0, concat_axis=0, tiled=True)  19.5 us
    all_to_all x1, waiting for transfers between devices, sum_at_owner(): lax.all_to_all(tiles, axis, split_axis=0, concat_axis=0, tiled=True)  17.9 us
    all_to_all x1, waiting for transfers between devices, on_device(): lax.all_to_all(kept_half, 'dp', split_axis=0, concat_axis=0, tiled=True)  11.9 us
    dot_general x1, matrix products, on_device(): jnp.dot(hidden_e, expert_down, preferred_element_type=jnp.float32)  11.2 us
  transfers between devices with their start and end apart: 9, of which 8 were waited for; matrix products, arithmetic and copies ran while one was open for 14% of the time, Pallas kernels for 0%

commit v1 on v0

--- a/solution.py
+++ b/solution.py
@@ -2,6 +2,11 @@
 import jax.numpy as jnp
 from jax import lax
 from jax.sharding import PartitionSpec as P
+
+
+def all_by_exchange(shard, axis, d):
+    sent = jnp.stack([shard] * lax.axis_size(axis))
+    return jnp.concatenate(lax.all_to_all(sent, axis, 0, 0), axis=d)
 
 
 def joined_along(tiles, dim):
@@ -78,9 +83,7 @@
     up_sum = jnp.dot(gathered, pieces[1], preferred_element_type=jnp.float32)
     shared_hidden = (jax.nn.silu(gate_sum) * up_sum).astype(jnp.bfloat16)
     shared_terms = jnp.dot(
-        shared_hidden,
-        lax.all_gather(shared_down, "dp", axis=1, tiled=True),
-        preferred_element_type=jnp.float32,
+        shared_hidden, all_by_exchange(shared_down, "dp", 1), preferred_element_type=jnp.float32
     )
     shared_out = lax.psum_scatter(
         shared_terms.astype(jnp.bfloat16), "tensor", scatter_dimension=1, tiled=True

time: 343 us -> 414 us (1.21); the launches traced: 343 us -> 408 us
  waiting for transfers between devices: 199 us -> 263 us
    all_to_all x1, waiting for transfers between devices: 17.9 us -> 89.3 us  [sum_at_owner(): lax.all_to_all(tiles, axis, split_axis=0, concat_axis=0, tiled=True)]
    all_to_all x0 -> x1, waiting for transfers between devices: none -> 56.9 us  [all_by_exchange(): return jnp.concatenate(lax.all_to_all(sent, axis, 0, 0), axis=d)]
    all_gather x1 -> x0, waiting for transfers between devices: 40.7 us -> none  [on_device(): lax.all_gather(shared_down, 'dp', axis=1, tiled=True)]
    all_gather x1, waiting for transfers between devices: 41 us -> 24 us  [side_by_side(): lax.all_gather(both, axis, axis=dim, tiled=True)]
    all_gather x1, waiting for transfers between devices: 63.9 us -> 57.1 us  [on_device(): portion = lax.all_gather(received, 'tensor', axis=2, tiled=True)]
    all_to_all x0 -> x1, starting transfers between devices: none -> 4.72 us  [all_by_exchange(): return jnp.concatenate(lax.all_to_all(sent, axis, 0, 0), axis=d)]
    unnamed x16 -> x20, local copies, waits for them, and re-layouts: 9.48 us -> 8.51 us
  transfers between devices with their start and end apart: 9 -> 9, of which waited for: 8 -> 8; matrix products, arithmetic and copies ran while one was open for 14% -> 12% of each run, Pallas kernels for 0% -> 0%
where the time goes in v1:
time: 414 us; the launch traced here: 408 us
  waiting for transfers between devices  263 us (64%)
  blocking collectives  40.7 us (10%)
  matrix products  32.2 us (8%)
  starting transfers between devices  25.3 us (6%)
  local copies, waits for them, and re-layouts  25 us (6%)
  between operations  13.3 us (3%)
  other arithmetic  9.23 us (2%)
    all_to_all x1, waiting for transfers between devices, sum_at_owner(): lax.all_to_all(tiles, axis, split_axis=0, concat_axis=0, tiled=True)  89.3 us
    all_gather x1, waiting for transfers between devices, on_device(): portion = lax.all_gather(received, 'tensor', axis=2, tiled=True)  57.1 us
    all_to_all x1, waiting for transfers between devices, all_by_exchange(): return jnp.concatenate(lax.all_to_all(sent, axis, 0, 0), axis=d)  56.9 us
    all_to_all x1, blocking collectives, on_device(): lax.all_to_all(to_send, 'dp', split_axis=0, concat_axis=0, tiled=True)  40.7 us
    all_gather x1, waiting for transfers between devices, side_by_side(): lax.all_gather(both, axis, axis=dim, tiled=True)  24 us
    all_to_all x1, waiting for transfers between devices, copy_for_each(): return lax.all_to_all(copies, axis, split_axis=0, concat_axis=0, tiled=True)  19.5 us
    all_to_all x1, waiting for transfers between devices, on_device(): lax.all_to_all(kept_half, 'dp', split_axis=0, concat_axis=0, tiled=True)  11.9 us
    dot_general x1, matrix products, on_device(): jnp.dot(hidden_e, expert_down, preferred_element_type=jnp.float32)  11.3 us
  transfers between devices with their start and end apart: 9, of which 8 were waited for; matrix products, arithmetic and copies ran while one was open for 12% of the time, Pallas kernels for 0%

profile of v1, /device:TPU:515, one launch (start us, length us, event | category | flops | bytes accessed | tf_op | source)
XLA Modules:
  0.0 408.3 jit_solution(3728576450878769849)
XLA Ops:
  6.6 1.2 copy.13
  7.8 1.3 broadcast_in_dim.8
  9.1 7.2 %all-to-all-start = ((bf16[8,128,640]{1,2,0:T(8,128)(2,1)}), bf16[8,128,640]{1,2,0:T(8,128)(2,1)}, u32[]{:S(2)}, u32[]{:S(2)}) async-start(bf16[8,128,640]{1,2,0:T(8,128)(2,1)} %broadcast_in_dim.8), calls=%async_computation | async-start | bytes 2621440 | tf_op jit(solution)/shard_map/all_to_all | solution.py:20
  16.2 19.5 %all-to-all-done = bf16[8,128,640]{1,2,0:T(8,128)(2,1)} async-done(((bf16[8,128,640]{1,2,0:T(8,128)(2,1)}), bf16[8,128,640]{1,2,0:T(8,128)(2,1)}, u32[]{:S(2)}, u32[]{:S(2)}) %all-to-all-start) | async-done | bytes 1310752 | tf_op jit(solution)/shard_map/all_to_all | solution.py:20
  35.7 1.6 fusion.17
  37.5 8.0 %scatter_fusion = bf16[8,32,640]{2,1,0:T(8,128)(2,1)S(1)} fusion(bf16[8,32,640]{2,1,0:T(8,128)(2,1)S(1)} %broadcast_in_dim.18, s32[128]{0:T(128)S(1)} %get-tuple-element.8, bf16[128,640]{1,0:T(8,128)(2,1)S(1)} %multiply_convert_fusion), kind=kCustom, calls=%fused_computation.1 | custom fusion | bytes 492544 | tf_op jit(solution)/shard_map/scatter | solution.py:79
  45.5 40.7 %all_to_all.25 = bf16[16,16,640]{2,1,0:T(8,128)(2,1)S(1)} all-to-all(bf16[16,16,640]{2,1,0:T(8,128)(2,1)S(1)} %bitcast.63), channel_id=1, replica_groups=mesh['group'=2,'dp'=16,'tensor'=8] {'dp'}, dimensions={0} | all-to-all | bytes 655360 | tf_op jit(solution)/shard_map/all_to_all | solution.py:93
  86.2 1.6 collective-permute-done
  87.9 0.9 pad_maximum_fusion.1
  88.9 2.0 pad_maximum_fusion
  91.0 2.8 stack.2
  93.8 4.7 %all-to-all-start.1 = ((bf16[16,512,320]{1,2,0:T(8,128)(2,1)}), bf16[16,512,320]{1,2,0:T(8,128)(2,1)}, u32[]{:S(2)}, u32[]{:S(2)}) async-start(bf16[16,512,320]{1,2,0:T(8,128)(2,1)} %stack.2), calls=%async_computation.1 | async-start | bytes 10485760 | tf_op jit(solution)/shard_map/all_to_all | solution.py:9
  98.6 57.1 %all-gather.5.cloned.1.call-done = bf16[16,32,5120]{2,1,0:T(8,128)(2,1)} async-done(((bf16[16,32,640]{2,1,0:T(8,128)(2,1)}), bf16[16,32,5120]{2,1,0:T(8,128)(2,1)}) %all-gather.5.cloned.1.call-update) | async-done | bytes 5242896 | tf_op jit(solution)/shard_map/all_gather | solution.py:103
  155.6 4.8 %fusion.40 = f32[512,256]{1,0:T(8,128)S(1)} fusion(bf16[512,5120]{1,0:T(8,128)(2,1)} %bitcast.68, bf16[5120,256]{1,0:T(8,128)(2,1)} %param.12), kind=kOutput, calls=%fused_computation.52 | convolution fusion | flops 1342177280 | bytes 8388608 | tf_op jit(solution)/shard_map/dot_general | solution.py:105
  160.5 11.3 %convolution_convert_fusion = bf16[512,5120]{1,0:T(8,128)(2,1)} fusion(bf16[256,5120]{1,0:T(8,128)(2,1)S(1)} %copy-done, bf16[512,5120]{1,0:T(8,128)(2,1)} %bitcast.69, bf16[5120,256]{1,0:T(8,128)(2,1)} %param.13, f32[512,256]{1,0:T(8,128)S(1)} %fusion.40), kind=kOutput, calls=%fused_computation.3 | convolution fusion | flops 2687762432 | bytes 16252928 | tf_op jit(solution)/shard_map/dot_general | solution.py:108
  171.8 3.7 copy.17
  175.4 3.0 copy.19
  178.5 56.9 %all-to-all-done.1 = bf16[16,512,320]{1,2,0:T(8,128)(2,1)} async-done(((bf16[16,512,320]{1,2,0:T(8,128)(2,1)}), bf16[16,512,320]{1,2,0:T(8,128)(2,1)}, u32[]{:S(2)}, u32[]{:S(2)}) %all-to-all-start.1) | async-done | bytes 5242912 | tf_op jit(solution)/shard_map/all_to_all | solution.py:9
  235.3 6.7 %all-to-all-start.3 = ((bf16[8,16,32,640]{3,2,1,0:T(8,128)(2,1)}), bf16[8,16,32,640]{3,2,1,0:T(8,128)(2,1)}, u32[]{:S(2)}, u32[]{:S(2)}) async-start(bf16[8,16,32,640]{3,2,1,0:T(8,128)(2,1)} %bitcast.61), calls=%async_computation.3 | async-start | bytes 10485760 | tf_op jit(solution)/shard_map/all_to_all | solution.py:43
  242.0 24.0 %all-gather.3.cloned.1.call-done = bf16[5120,1024]{1,0:T(8,128)(2,1)} async-done(((bf16[320,1024]{1,0:T(8,128)(2,1)}), bf16[5120,1024]{1,0:T(8,128)(2,1)}) %all-gather.3.cloned.1.call-update) | async-done | bytes 10485776 | tf_op jit(solution)/shard_map/all_gather | solution.py:29
  266.0 4.4 %fusion.5 = f32[128,512]{0,1:T(8,128)S(1)} fusion(bf16[128,5120]{0,1:T(8,128)(2,1)} %bitcast.1, bf16[5120,1024]{1,0:T(8,128)(2,1)} %all-gather.3.cloned.1.call-done), kind=kOutput, calls=%fused_computation.12 | convolution fusion | flops 671088640 | bytes 6815744 | tf_op jit(solution)/shard_map/dot_general | solution.py:82
  270.4 10.1 %convolution_convert_fusion.1 = bf16[128,5120]{1,0:T(8,128)(2,1)S(1)} fusion(bf16[512,5120]{0,1:T(8,128)(2,1)} %bitcast.6, bf16[128,5120]{0,1:T(8,128)(2,1)} %bitcast.1, bf16[5120,1024]{1,0:T(8,128)(2,1)} %all-gather.3.cloned.1.call-done, f32[128,512]{0,1:T(8,128)S(1)} %fusion.5), kind=kOutput, calls=%fused_computation.4 | convolution fusion | flops 1343225856 | bytes 13369344 | tf_op jit(solution)/shard_map/dot_general | solution.py:85
  280.6 1.5 copy.15
  282.1 89.3 %all-to-all-done.3 = bf16[8,16,32,640]{3,2,1,0:T(8,128)(2,1)} async-done(((bf16[8,16,32,640]{3,2,1,0:T(8,128)(2,1)}), bf16[8,16,32,640]{3,2,1,0:T(8,128)(2,1)}, u32[]{:S(2)}, u32[]{:S(2)}) %all-to-all-start.3) | async-done | bytes 5242912 | tf_op jit(solution)/shard_map/all_to_all | solution.py:43
  371.4 3.4 convert_reduce_fusion
  374.8 1.1 copy-done.2
  376.1 2.2 collective-permute-done.1
  378.3 2.0 fusion.20
  380.2 6.5 %all-to-all-start.4 = ((bf16[16,16,640]{2,1,0:T(8,128)(2,1)}), bf16[16,16,640]{2,1,0:T(8,128)(2,1)S(1)}, u32[]{:S(2)}, u32[]{:S(2)}) async-start(bf16[16,16,640]{2,1,0:T(8,128)(2,1)} %fusion.20), calls=%async_computation.4 | async-start | bytes 655360 | tf_op jit(solution)/shard_map/all_to_all | solution.py:116
  386.7 1.1 copy.16
  387.8 11.9 %all-to-all-done.4 = bf16[16,16,640]{2,1,0:T(8,128)(2,1)S(1)} async-done(((bf16[16,16,640]{2,1,0:T(8,128)(2,1)}), bf16[16,16,640]{2,1,0:T(8,128)(2,1)S(1)}, u32[]{:S(2)}, u32[]{:S(2)}) %all-to-all-start.4) | async-done | bytes 327712 | tf_op jit(solution)/shard_map/all_to_all | solution.py:116
  399.7 1.4 gather_fusion
  (31 shorter events, 1.4 us)
Async XLA Ops:
  6.5 153.9 %copy-start = (bf16[256,5120]{1,0:T(8,128)(2,1)S(1)}, bf16[256,5120]{1,0:T(8,128)(2,1)}, u32[]{:S(2)}) copy-start(bf16[256,5120]{1,0:T(8,128)(2,1)} %param.14) | copy-start | bytes 7864324
  6.6 9.7 %copy-start.7 = (s32[128]{0:T(128)S(1)}, s32[128]{0:T(128)}, u32[]{:S(2)}) copy-start(s32[128]{0:T(128)} %param.19) | copy-start | bytes 1540
  6.6 9.7 %copy-start.6 = (s32[128]{0:T(128)S(1)}, s32[128]{0:T(128)}, u32[]{:S(2)}) copy-start(s32[128]{0:T(128)} %param.18) | copy-start | bytes 1540
  6.6 29.2 %copy-start.5 = (bf16[5120,8]{0,1:T(8,128)(2,1)S(1)}, bf16[5120,8]{0,1:T(8,128)(2,1)}, u32[]{:S(2)}) copy-start(bf16[5120,8]{0,1:T(8,128)(2,1)} %param.11) | copy-start | bytes 245764
  7.8 29.6 %copy-start.3 = (bf16[128,640]{1,0:T(8,128)(2,1)S(1)}, bf16[128,640]{1,0:T(8,128)(2,1)}, u32[]{:S(2)}) copy-start(bf16[128,640]{1,0:T(8,128)(2,1)} %param.10) | copy-start | bytes 491524
  9.1 26.6 %all-to-all-start = ((bf16[8,128,640]{1,2,0:T(8,128)(2,1)}), bf16[8,128,640]{1,2,0:T(8,128)(2,1)}, u32[]{:S(2)}, u32[]{:S(2)}) async-start(bf16[8,128,640]{1,2,0:T(8,128)(2,1)} %broadcast_in_dim.8), calls=%async_computation | async-start | bytes 2621440 | tf_op jit(solution)/shard_map/all_to_all | solution.py:20
  16.2 139.4 %all-gather.5.cloned.1.call-start = ((), (), s32[]{:S(2)}) async-start(), calls=%async_computation.7 | async-start | bytes 5898240 | tf_op jit(solution)/shard_map/all_gather | solution.py:103
  86.2 1.6 collective-permute-start
  87.9 3.1 copy-start.4
  88.8 177.2 %all-gather.3.cloned.1.call-start = ((), (), s32[]{:S(2)}) async-start(), calls=%async_computation.6 | async-start | bytes 11141120 | tf_op jit(solution)/shard_map/all_gather | solution.py:29
  93.8 141.5 %all-to-all-start.1 = ((bf16[16,512,320]{1,2,0:T(8,128)(2,1)}), bf16[16,512,320]{1,2,0:T(8,128)(2,1)}, u32[]{:S(2)}, u32[]{:S(2)}) async-start(bf16[16,512,320]{1,2,0:T(8,128)(2,1)} %stack.2), calls=%async_computation.1 | async-start | bytes 10485760 | tf_op jit(solution)/shard_map/all_to_all | solution.py:9
  235.3 136.0 %all-to-all-start.3 = ((bf16[8,16,32,640]{3,2,1,0:T(8,128)(2,1)}), bf16[8,16,32,640]{3,2,1,0:T(8,128)(2,1)}, u32[]{:S(2)}, u32[]{:S(2)}) async-start(bf16[8,16,32,640]{3,2,1,0:T(8,128)(2,1)} %bitcast.61), calls=%async_computation.3 | async-start | bytes 10485760 | tf_op jit(solution)/shard_map/all_to_all | solution.py:43
  242.0 144.7 %reduce-scatter.4.cloned.1.call-start = ((), (), s32[]{:S(2)}) async-start(), calls=%async_computation.8 | async-start | bytes 1474560
  374.8 1.1 copy-start.2
  375.8 26.0 %copy-start.1 = (bf16[256,5120]{1,0:T(8,128)(2,1)S(1)}, bf16[256,5120]{1,0:T(8,128)(2,1)}, u32[]{:S(2)}) copy-start(bf16[256,5120]{1,0:T(8,128)(2,1)} %param.14) | copy-start | bytes 7864324
  375.9 2.4 collective-permute-start.1
  380.2 19.5 %all-to-all-start.4 = ((bf16[16,16,640]{2,1,0:T(8,128)(2,1)}), bf16[16,16,640]{2,1,0:T(8,128)(2,1)S(1)}, u32[]{:S(2)}, u32[]{:S(2)}) async-start(bf16[16,16,640]{2,1,0:T(8,128)(2,1)} %fusion.20), calls=%async_computation.4 | async-start | bytes 655360 | tf_op jit(solution)/shard_map/all_to_all | solution.py:116
Sparse Core Ops, SparseCore 0:
  89.0 66.6 all-gather.4
  157.5 108.4 all-gather.2
  282.2 64.0 reduce-scatter.3
